TPU v7x, 128 devices: a whole 4x4x4 slice. The times are simulated.
128 devices in a mesh: panel: 16 (over z, x), prb: 8 (over y, core).
Axes of the slice: x: 4, y: 4, z: 4, core: 2. Of those that a mesh axis runs over, the one named last changes fastest.
Arguments:
- channel: bfloat16 [224, 256, 64, 128], P('panel', 'prb'), may hold values from -0.125 to 0.125
- received: bfloat16 [224, 256, 64, 288], P('panel', 'prb'), may hold values from -6 to 6
- keep_list: int32 [224, 256, 3], P('panel', 'prb'), may hold values from 0 to 4, as said below
- alloc: int32 [256, 64], replicated, may hold values from 0 to 511, all different within a row
- noise_var: float32 [512], replicated, may hold values from 0.1 to 1
- owner: int32 [256, 64, 1], replicated, may hold values from 0 to 127; in each aligned block of 128 rows (0 to 127, 128 to 255, ..., all dimensions but the last counted through in order) at most 2 rows name the same one
Outputs:
- equalized: float32 [32768, 288], P(('panel', 'prb'))
Inputs may be any that keep to these rules, and one draw needn't show every extreme that they name: `keep_list`: entries below 4 name distinct beam blocks of the panel; entries equal to 4 are empty slots and stand after the kept ones; each panel keeps between 1 and 3 blocks for each PRB. `alloc`: each PRB lists 64 different users, and every user is listed by some PRB. Owners are device numbers along panel+prb. In each aligned block of 128 rows (PRB-major, then layer), no owner appears more than 2 times.
All inputs are finite; a program needn't handle non-finite values.
Results may differ from a plain program's by a relative error of at most 0.005.
Values may be sent and summed in bfloat16 or wider, within the bound.
No kernel may reach another device: no remote copies, remote signals or barrier semaphores. Data moves between devices by JAX's collectives and lax.ppermute only.
A program may use at most 192 MiB of HBM per device.

v0:
```python
import math

import jax
import jax.numpy as jnp
from jax import lax
from jax.sharding import PartitionSpec as P

ANTENNA_EDGE = 8
NBLK = 4


def in_blocks(shard, dim, length):
    lengths = shard.shape
    parts = shard.reshape(*lengths[:dim], length, lengths[dim] // length, *lengths[dim + 1 :])
    return jnp.moveaxis(parts, dim, 0)


def summed_on_arrival(shard, axis, dim):
    parts = in_blocks(shard, dim, lax.axis_size(axis))
    arrived = lax.all_to_all(parts, axis, split_axis=0, concat_axis=0, tiled=True)
    return arrived.astype(jnp.float32).sum(axis=0)


def laid_out(parts, dim):
    parts = jnp.moveaxis(parts, 0, dim)
    lengths = parts.shape
    return parts.reshape(*lengths[:dim], lengths[dim] * lengths[dim + 1], *lengths[dim + 2 :])


def joined_exchange(shard, axis, axes, splits, concats):
    sizes = [lax.axis_size(a) for a in axes]
    parts = in_blocks(shard, splits[0], sizes[0])
    parts = jnp.moveaxis(in_blocks(parts, splits[1] + 1, sizes[1]), 0, 1)
    inside = parts.shape[2:]
    parts = parts.reshape(-1, *inside)
    parts = lax.all_to_all(parts, axis, split_axis=0, concat_axis=0, tiled=True)
    parts = laid_out(parts.reshape(*sizes, *inside), concats[0] + 1)
    return laid_out(parts, concats[1])


def beamspace_tables(panel_side):
    length = panel_side * panel_side
    positions = jnp.arange(length, dtype=jnp.int32)
    first_axis = positions // panel_side
    second_axis = positions % panel_side
    phases = (
        first_axis[:, None] * first_axis[None, :] + second_axis[:, None] * second_axis[None, :]
    ) % panel_side
    angles = phases.astype(jnp.float32) * (2.0 * math.pi / panel_side)
    real_part = (jnp.cos(angles) / panel_side).astype(jnp.bfloat16)
    imag_part = (-jnp.sin(angles) / panel_side).astype(jnp.bfloat16)
    return (real_part, imag_part)


def combine_parts(first, second, width):
    return jnp.concatenate(
        [first[..., :width] - second[..., width:], second[..., :width] + first[..., width:]],
        axis=-1,
    ).astype(jnp.bfloat16)


def solve_one(factor_one, right_one):
    return jax.scipy.linalg.cho_solve((factor_one, True), right_one)


def solve_layers(products, noise, layer_count, res_count):
    block_a = products[:, :layer_count, :layer_count]
    block_b = products[:, :layer_count, layer_count : 2 * layer_count]
    block_c = products[:, layer_count : 2 * layer_count, :layer_count]
    block_d = products[:, layer_count : 2 * layer_count, layer_count : 2 * layer_count]
    identity = jnp.eye(layer_count, dtype=jnp.float32)
    gram_real = block_a + block_d + identity[None] * noise[:, :, None]
    gram_imag = block_b - block_c
    system = jnp.concatenate(
        [jnp.concatenate([gram_real, -gram_imag], 2), jnp.concatenate([gram_imag, gram_real], 2)], 1
    )
    matched = products[:, :, 2 * layer_count :]
    match_real = matched[:, :layer_count, :res_count] + matched[:, layer_count:, res_count:]
    match_imag = matched[:, :layer_count, res_count:] - matched[:, layer_count:, :res_count]
    right_side = jnp.concatenate([match_real, match_imag], 1)
    factor = jnp.linalg.cholesky(system)
    solved = jax.vmap(solve_one)(factor, right_side)
    rows = jnp.concatenate([solved[:, :layer_count], solved[:, layer_count:]], 2)
    return rows.reshape(-1, 2 * res_count)


def panel_beams(
    channel_panel,
    signal_panel,
    keep_panel,
    beam_table_real,
    beam_table_imag,
    layer_count,
    res_count,
):
    blocks = NBLK
    block_size = beam_table_real.shape[0] // blocks
    selector = (
        keep_panel[:, :, None] == jnp.arange(blocks, dtype=jnp.int32)[None, None, :]
    ).astype(jnp.bfloat16)

    def pick_rows(table):
        shaped = table.reshape(blocks, block_size, table.shape[1])
        chosen = jnp.einsum("pkb,bja->pkja", selector, shaped, preferred_element_type=jnp.float32)
        return chosen.reshape(chosen.shape[0], -1, table.shape[1]).astype(jnp.bfloat16)

    rows_real = pick_rows(beam_table_real)
    rows_imag = pick_rows(beam_table_imag)

    def apply_rows(signal, width):
        first = jnp.einsum("pqa,pac->pqc", rows_real, signal, preferred_element_type=jnp.float32)
        second = jnp.einsum("pqa,pac->pqc", rows_imag, signal, preferred_element_type=jnp.float32)
        return combine_parts(first, second, width)

    return jnp.concatenate(
        [apply_rows(channel_panel, layer_count), apply_rows(signal_panel, res_count)], axis=-1
    )


def route_rows(rows, owner_rows, devices, capacity):
    highest = lax.Precision.HIGHEST
    total = rows.shape[0]
    onehot = (owner_rows[:, None] == jnp.arange(devices, dtype=jnp.int32)[None, :]).astype(
        jnp.float32
    )
    earlier = (jnp.arange(total)[:, None] > jnp.arange(total)[None, :]).astype(jnp.float32)
    counts = jnp.dot(earlier, onehot, precision=highest)
    slots = jnp.sum(counts * onehot, axis=1)
    place = onehot[:, :, None] * (
        slots[:, None, None] == jnp.arange(capacity).astype(jnp.float32)[None, None, :]
    ).astype(jnp.float32)
    return jnp.einsum("rdk,rc->dkc", place, rows, precision=highest)


def body(channel, received, keep_list, alloc, noise_var, owner):
    beam_table_real, beam_table_imag = beamspace_tables(ANTENNA_EDGE)
    layer_count = channel.shape[-1] // 2
    res_count = received.shape[-1] // 2

    def per_panel(items):
        return panel_beams(
            items[0], items[1], items[2], beam_table_real, beam_table_imag, layer_count, res_count
        )

    kept = lax.map(per_panel, (channel, received, keep_list))
    panel_count = lax.axis_size("panel")
    prb_count = lax.axis_size("prb")
    prb_local = channel.shape[1]
    prb_own = prb_local // panel_count
    products = summed_on_arrival(
        jnp.einsum(
            "mkqc,mkqd->kcd", kept[..., : 2 * layer_count], kept, preferred_element_type=jnp.float32
        ).astype(jnp.bfloat16),
        "panel",
        0,
    )
    first_prb = lax.axis_index("prb") * prb_local + lax.axis_index("panel") * prb_own
    alloc_rows = lax.dynamic_slice_in_dim(alloc, first_prb, prb_own, 0)
    owner_rows = lax.dynamic_slice_in_dim(owner, first_prb, prb_own, 0).reshape(-1)
    matches = (
        alloc_rows[:, :, None] == jnp.arange(noise_var.shape[0], dtype=jnp.int32)[None, None, :]
    )
    noise = jnp.sum(jnp.where(matches, noise_var[None, None, :], jnp.float32(0.0)), axis=-1)
    layer_rows = solve_layers(products, noise, layer_count, res_count)
    devices = panel_count * prb_count
    capacity = max(2, 2 * prb_own * layer_count // devices)
    outgoing = route_rows(layer_rows, owner_rows, devices, capacity)
    shaped = outgoing.reshape(panel_count, prb_count, capacity, outgoing.shape[-1])
    arrived = joined_exchange(shaped, ("panel", "prb"), ("panel", "prb"), (0, 1), (0, 1))
    return arrived.reshape(-1, outgoing.shape[-1])


def solution(mesh):
    placed = (
        P("panel", "prb", None, None),
        P("panel", "prb", None, None),
        P("panel", "prb", None),
        P(),
        P(),
        P(),
    )
    return jax.shard_map(
        body, mesh=mesh, in_specs=placed, out_specs=P(("panel", "prb"), None), check_vma=False
    )
```

profile of v0, /device:TPU:1, one launch (start us, length us, event | category | flops | bytes accessed | tf_op | source)
XLA Modules:
  0.0 306.8 jit_solution(15404211665176595992)
XLA Ops:
  0.0 164.9 %while.12 = (s32[]{:T(128)}, bf16[14,32,48,416]{3,2,0,1:T(8,128)(2,1)}, s32[14,32,3]{1,0,2:T(8,128)}, bf16[14,32,64,128]{3,2,1,0:T(8,128)(2,1)}, bf16[14,32,64,2...) while((s32[]{:T(128)}, ...), condition=%wide.region_2.3_spmd.clone.clone, body=%wide.region_1.2_spmd.clone.clone.sunk | while | flops 171823872 | bytes 19762036 | solution.py:145
  1.3 2.0 fusion.98
  3.7 2.0 fusion.99
  45.1 2.0 fusion.104
  56.9 2.0 fusion.104
  68.7 2.0 fusion.104
  72.0 2.0 fusion.98
  92.2 2.0 fusion.104
  95.5 2.0 fusion.98
  104.0 2.0 fusion.104
  115.8 2.0 fusion.104
  119.1 2.0 fusion.98
  121.4 2.0 fusion.99
  130.8 2.0 fusion.98
  133.2 2.0 fusion.99
  139.3 2.0 fusion.104
  151.1 2.0 fusion.104
  163.0 2.0 fusion.104
  164.9 13.6 %bitcast_convert_fusion = bf16[32,128,416]{1,2,0:T(8,128)(2,1)} fusion(bf16[14,32,48,416]{3,2,0,1:T(8,128)(2,1)} %get-tuple-element.42), kind=kOutput, calls=%fused_computation.52 | convolution fusion | flops 2291793920 | bytes 30932992 | tf_op jit(solution)/shard_map/mkqc,mkqd->kcd/dot_general | solution.py:151
  178.6 8.4 %all-to-all-start = ((bf16[16,2,128,416]{2,3,1,0:T(8,128)(2,1)}), bf16[16,2,128,416]{2,3,1,0:T(8,128)(2,1)S(1)}, u32[]{:S(2)}, u32[]{:S(2)}) async-start(bf16[16,2,128,416]{2,3,1,0:T(8,128)(2,1)} %bitcast.2), calls=%async_computation | async-start | bytes 6815744 | tf_op jit(solution)/shard_map/all_to_all | solution.py:20
  195.2 42.4 %all-to-all-done = bf16[16,2,128,416]{2,3,1,0:T(8,128)(2,1)S(1)} async-done(((bf16[16,2,128,416]{2,3,1,0:T(8,128)(2,1)}), bf16[16,2,128,416]{2,3,1,0:T(8,128)(2,1)S(1)}, u32[]{:S(2)}, u32[]{:S(2)}) %all-to-all-start) | async-done | bytes 3407904 | tf_op jit(solution)/shard_map/all_to_all | solution.py:20
  238.9 23.5 %custom-call.11 = f32[2,128,128]{2,1,0:T(8,128)S(1)} custom-call(f32[2,128,128]{2,1,0:T(8,128)S(1)} %fusion.53), custom_call_target="Cholesky" | custom-call | tf_op jit(solution)/shard_map/jit(cholesky)/cholesky | solution.py:81
  263.3 19.7 %custom-call.12 = f32[2,1,128,128]{2,3,1,0:T(8,128)S(1)} custom-call(f32[2,1,128,128]{3,2,1,0:T(8,128)S(1)} %select_bitcast_fusion), custom_call_target="InvertDiagBlocksLowerTriangular" | custom-call | tf_op jit(solution)/shard_map/vmap(jit(_cho_solve))/triangular_solve | solution.py:63
  284.8 20.5 %all_to_all.10 = f32[128,1,1,2,288]{4,3,2,1,0:T(2,128)S(1)} all-to-all(f32[128,1,1,2,288]{4,3,2,1,0:T(2,128)S(1)} %copy.75), channel_id=1, replica_groups=mesh['panel'=16,'prb'=8] {'panel','prb'}, dimensions={0} | all-to-all | bytes 589824 | tf_op jit(solution)/shard_map/all_to_all | solution.py:36
  (197 shorter events, 143.8 us)
Async XLA Ops:
  0.0 187.0 %copy-start = (s32[256,64]{0,1:T(8,128)S(1)}, s32[256,64]{0,1:T(8,128)}, u32[]{:S(2)}) copy-start(s32[256,64]{0,1:T(8,128)} %param.11) | copy-start | bytes 196612
  178.6 59.1 %all-to-all-start = ((bf16[16,2,128,416]{2,3,1,0:T(8,128)(2,1)}), bf16[16,2,128,416]{2,3,1,0:T(8,128)(2,1)S(1)}, u32[]{:S(2)}, u32[]{:S(2)}) async-start(bf16[16,2,128,416]{2,3,1,0:T(8,128)(2,1)} %bitcast.2), calls=%async_computation | async-start | bytes 6815744 | tf_op jit(solution)/shard_map/all_to_all | solution.py:20
  188.8 0.6 copy-start.4
  237.7 0.8 copy-start.1
  237.7 0.8 copy-start.3
  238.1 45.9 %copy-start.2 = (f32[128,2]{0,1:T(2,128)S(1)}, f32[128,2]{0,1:T(2,128)}, u32[]{:S(2)}) copy-start(f32[128,2]{0,1:T(2,128)} %compare_convert_fusion) | copy-start | bytes 3076
where the time goes:
time: 310 us; the launch traced here: 307 us
  matrix products  120 us (39%)
  other arithmetic  98.9 us (32%)
  waiting for transfers between devices  42.4 us (14%)
  blocking collectives  20.5 us (7%)
  local copies, waits for them, and re-layouts  15.6 us (5%)
  starting transfers between devices  8.42 us (3%)
    dot_general x28, matrix products, apply_rows(): jnp.einsum('pqa,pac->pqc', rows_imag, signal, preferred_element_type=jnp....  47.2 us
    dot_general x28, matrix products, apply_rows(): jnp.einsum('pqa,pac->pqc', rows_real, signal, preferred_element_type=jnp....  47.2 us
    all_to_all x1, waiting for transfers between devices, summed_on_arrival(): lax.all_to_all(parts, axis, split_axis=0, concat_axis=0, tiled=True)  42.4 us
    dynamic_update_slice x14, other arithmetic, body(): kept = lax.map(per_panel, (channel, received, keep_list))  27.8 us
    another operation x4, other arithmetic, solve_layers(): factor = jnp.linalg.cholesky(system)  24.9 us
    all_to_all x1, blocking collectives, joined_exchange(): parts = lax.all_to_all(parts, axis, split_axis=0, concat_axis=0, tiled=True)  20.5 us
    another operation x3, other arithmetic, solve_one(): return jax.scipy.linalg.cho_solve((factor_one, True), right_one)  19.8 us
    another operation x28, other arithmetic  19.1 us
  transfers between devices with their start and end apart: 1, of which 1 were waited for; matrix products, arithmetic and copies ran while one was open for 2% of the time, Pallas kernels for 0%

commit v1 on v0

v1 whole, which is shorter than its diff:
```python
import jax
import jax.numpy as jnp
import ml_dtypes
import numpy as np
from jax import lax
from jax.experimental import pallas as pl
from jax.experimental.pallas import tpu as pltpu
from jax.sharding import PartitionSpec as P

EDGE = 8
ANT = EDGE * EDGE
NBLK = 4
LAYERS = 64
RES = 144
PACK = 384


def projector_tables():
    pos = np.arange(ANT)
    first, second = pos // EDGE, pos % EDGE
    phase = (first[:, None] * first[None, :] + second[:, None] * second[None, :]) % EDGE
    cos8 = np.array([1.0, np.sqrt(0.5), 0.0, -np.sqrt(0.5), -1.0, -np.sqrt(0.5), 0.0, np.sqrt(0.5)])
    sin8 = np.array([0.0, np.sqrt(0.5), 1.0, np.sqrt(0.5), 0.0, -np.sqrt(0.5), -1.0, -np.sqrt(0.5)])
    real = (cos8[phase] / EDGE).astype(ml_dtypes.bfloat16).astype(np.float64)
    imag = (-sin8[phase] / EDGE).astype(ml_dtypes.bfloat16).astype(np.float64)
    beams = real + 1j * imag
    table = np.zeros((2, 1 << NBLK, ANT, 4 * ANT), np.float64)
    rows = ANT // NBLK
    for pattern in range(1 << NBLK):
        keep = np.array([(pattern >> (q // rows)) & 1 for q in range(ANT)], np.float64)
        proj = np.conj(beams.T) @ (keep[:, None] * beams)
        for half in range(2):
            table[half, pattern, :, half * ANT : (half + 1) * ANT] = proj.real
            table[half, pattern, :, (2 + half) * ANT : (3 + half) * ANT] = proj.imag
    return table.astype(ml_dtypes.bfloat16)


TABLE = projector_tables()


def rotated(m, width):
    return jnp.concatenate([m[:, width:], -m[:, :width]], axis=1)


def sums_kernel(pats_ref, table_ref, ch_ref, rx_ref, out_ref, *, panels, prbs, steps_prb):
    step = pl.program_id(0)
    for j in range(prbs):
        p = step * prbs + j
        pieces = []
        for n in range(0, panels, 2):
            pair = ch_ref[n : n + 2, j].reshape(2 * ANT, 2 * LAYERS)
            weights = jnp.concatenate(
                [
                    table_ref[0, pats_ref[n * steps_prb + p]],
                    table_ref[1, pats_ref[(n + 1) * steps_prb + p]],
                ],
                axis=0,
            )
            ab = jnp.dot(pair.T, weights, preferred_element_type=jnp.float32)
            a, b = ab[:, : 2 * ANT], ab[:, 2 * ANT :]
            pieces.append(
                jnp.concatenate(
                    [a[:LAYERS] + b[LAYERS:], a[LAYERS:] - b[:LAYERS]], axis=0
                ).astype(jnp.bfloat16)
            )
        left = jnp.concatenate(pieces, axis=1)
        ch = ch_ref[:, j].reshape(panels * ANT, 2 * LAYERS)
        rx = rx_ref[:, j].reshape(panels * ANT, 2 * RES)
        head = jnp.dot(left, rx[:, :256], preferred_element_type=jnp.float32)
        rest = jnp.dot(
            left, jnp.concatenate([ch, rx[:, 256:]], axis=1), preferred_element_type=jnp.float32
        )
        my = jnp.concatenate([head, rest[:, 128:]], axis=1)
        mh = rest[:, :128]
        z = my[:LAYERS] + rotated(my[LAYERS:], RES)
        g = mh[:LAYERS] + rotated(mh[LAYERS:], LAYERS)
        swapped = pltpu.roll(g, LAYERS, axis=1)
        row = lax.broadcasted_iota(jnp.int32, (LAYERS, 128), 0)
        lane = lax.broadcasted_iota(jnp.int32, (LAYERS, 128), 1)
        packed = jnp.where(row >= lane - LAYERS, swapped, g)
        out_ref[j, :, :256] = z[:, :256].astype(jnp.bfloat16)
        tail = jnp.concatenate([z[:, 256:], jnp.zeros((LAYERS, 96), jnp.float32)], axis=1)
        out_ref[j, :, 256:] = jnp.where(lane >= LAYERS, packed, tail).astype(jnp.bfloat16)


def panel_sums(pats, channel, received):
    panels, prb_local = channel.shape[:2]
    prbs = 2
    import functools

    kernel = functools.partial(sums_kernel, panels=panels, prbs=prbs, steps_prb=prb_local)
    return pl.pallas_call(
        kernel,
        grid_spec=pltpu.PrefetchScalarGridSpec(
            num_scalar_prefetch=1,
            grid=(prb_local // prbs,),
            in_specs=[
                pl.BlockSpec(TABLE.shape, lambda i, s: (0, 0, 0, 0)),
                pl.BlockSpec((panels, prbs, ANT, 2 * LAYERS), lambda i, s: (0, i, 0, 0)),
                pl.BlockSpec((panels, prbs, ANT, 2 * RES), lambda i, s: (0, i, 0, 0)),
            ],
            out_specs=pl.BlockSpec((prbs, LAYERS, PACK), lambda i, s: (i, 0, 0)),
        ),
        out_shape=jax.ShapeDtypeStruct((prb_local, LAYERS, PACK), jnp.bfloat16),
        compiler_params=pltpu.CompilerParams(dimension_semantics=("arbitrary",)),
        name="panel_sums",
    )(pats, jnp.asarray(TABLE), channel, received)


def solve_kernel(arr_ref, noise_ref, place_ref, out_ref, *, sources):
    def total(j):
        acc = arr_ref[0, j].astype(jnp.float32)
        for s in range(1, sources):
            acc = acc + arr_ref[s, j].astype(jnp.float32)
        return acc

    s0, s1 = total(0), total(1)
    row = lax.broadcasted_iota(jnp.int32, (LAYERS, 128), 0)
    lane = lax.broadcasted_iota(jnp.int32, (LAYERS, 128), 1)
    upper = lane >= LAYERS
    col = jnp.where(upper, lane - LAYERS, lane)
    q = jnp.where(upper, s1[:, 256:], pltpu.roll(s0[:, 256:], LAYERS, axis=1))
    qt = jnp.concatenate([q, jnp.zeros_like(q)], axis=0).T
    qt = jnp.where(upper, pltpu.roll(qt[LAYERS:], LAYERS, axis=1), qt[:LAYERS])
    ar = jnp.where(row >= col, q, qt) + jnp.where(row == col, noise_ref[...], 0.0)
    ai = jnp.where(col > row, q, jnp.where(col < row, -qt, 0.0))
    base = jnp.where(upper, LAYERS, 0)
    for k in range(LAYERS):
        idx = base + k
        cr = jnp.take_along_axis(ar, idx, axis=1, mode="promise_in_bounds")
        ci = jnp.take_along_axis(ai, idx, axis=1, mode="promise_in_bounds")
        inv = 1.0 / cr[k : k + 1]
        here = col == k
        ar = jnp.where(here, 0.0, ar)
        ai = jnp.where(here, 0.0, ai)
        rr = jnp.where(here[:1], inv, ar[k : k + 1] * inv)
        ri = ai[k : k + 1] * inv
        ar = ar - (cr * rr - ci * ri)
        ai = ai - (cr * ri + ci * rr)
        this = row == k
        ar = jnp.where(this, rr, ar)
        ai = jnp.where(this, ri, ai)
    z = jnp.concatenate([s0[:, : 2 * RES], s1[:, : 2 * RES]], axis=0)
    rows = []
    for half in (~upper, upper):
        left = jnp.concatenate([jnp.where(half, ar, 0.0), jnp.where(half, ai, 0.0)], axis=0)
        r = jnp.dot(left, z, precision=lax.Precision.HIGHEST, preferred_element_type=jnp.float32)
        rows.append(r[:LAYERS] - rotated(r[LAYERS:], RES))
    x = jnp.concatenate(rows, axis=0).astype(jnp.bfloat16)
    out_ref[...] = jnp.dot(place_ref[...], x, preferred_element_type=jnp.float32).astype(jnp.bfloat16)


def solve_and_route(arrived, noise, place):
    import functools

    return pl.pallas_call(
        functools.partial(solve_kernel, sources=arrived.shape[0]),
        out_shape=jax.ShapeDtypeStruct((place.shape[0], 2 * RES), jnp.bfloat16),
        name="solve_and_route",
    )(arrived, noise, place)


def body(channel, received, keep_list, alloc, noise_var, owner):
    panel_count = lax.axis_size("panel")
    prb_count = lax.axis_size("prb")
    prb_local = channel.shape[1]
    prb_own = prb_local // panel_count
    pats = jnp.sum(jnp.where(keep_list < NBLK, 1 << keep_list, 0), axis=-1).astype(jnp.int32)
    sums = panel_sums(pats.reshape(-1), channel, received)
    parts = sums.reshape(panel_count, prb_own, LAYERS, PACK)
    arrived = lax.all_to_all(parts, "panel", split_axis=0, concat_axis=0, tiled=True)

    first_prb = lax.axis_index("prb") * prb_local + lax.axis_index("panel") * prb_own
    alloc_rows = lax.dynamic_slice_in_dim(alloc, first_prb, prb_own, 0)
    owner_rows = lax.dynamic_slice_in_dim(owner, first_prb, prb_own, 0).reshape(-1)
    users = jnp.arange(noise_var.shape[0], dtype=jnp.int32)
    matches = alloc_rows[:, :, None] == users[None, None, :]
    noise = jnp.sum(jnp.where(matches, noise_var[None, None, :], jnp.float32(0.0)), axis=-1)
    devices = panel_count * prb_count
    capacity = 2
    total = owner_rows.shape[0]
    same = owner_rows[:, None] == owner_rows[None, :]
    before = jnp.arange(total)[:, None] < jnp.arange(total)[None, :]
    slots = jnp.sum(jnp.where(same & before, 1, 0), axis=0)
    target = owner_rows * capacity + slots
    place = (jnp.arange(devices * capacity)[:, None] == target[None, :]).astype(jnp.bfloat16)

    outgoing = solve_and_route(arrived, noise.reshape(1, -1), place)
    shaped = outgoing.reshape(devices, capacity, 2 * RES)
    final = lax.all_to_all(shaped, ("panel", "prb"), split_axis=0, concat_axis=0, tiled=True)
    return final.reshape(-1, 2 * RES).astype(jnp.float32)


def solution(mesh):
    placed = (
        P("panel", "prb", None, None),
        P("panel", "prb", None, None),
        P("panel", "prb", None),
        P(),
        P(),
        P(),
    )
    return jax.shard_map(
        body, mesh=mesh, in_specs=placed, out_specs=P(("panel", "prb"), None), check_vma=False
    )
```

time: 310 us -> 85.9 us (0.28)
  matrix products: 120 us -> 0 us
  other arithmetic: 98.9 us -> 1.73 us
  Pallas kernels: 0 us -> 31.4 us
  waiting for transfers between devices: 42.4 us -> 21.1 us
  local copies, waits for them, and re-layouts: 15.6 us -> 4.84 us
    dot_general x87 -> x0, matrix products: 119 us -> none  [the longest x28 47.2 us: apply_rows(): jnp.einsum('pqa,pac->pqc', rows_imag, signal, preferred_element_type=jnp....]
    another operation x35 -> x0, other arithmetic: 63.8 us -> none  [the longest x4 24.9 us: solve_layers(): factor = jnp.linalg.cholesky(system)]
    pallas_call x0 -> x2, Pallas kernels: none -> 31.4 us  [the longest x1 22.6 us: panel_sums(): pl.pallas_call(kernel, grid_spec=pltpu.PrefetchScalarGridSpec(num_scalar_...]
    dynamic_update_slice x14 -> x0, other arithmetic: 27.8 us -> none  [body(): kept = lax.map(per_panel, (channel, received, keep_list))]
    all_to_all x1, waiting for transfers between devices: 42.4 us -> 21.1 us  [body(): lax.all_to_all(parts, 'panel', split_axis=0, concat_axis=0, tiled=True)]
    dynamic_slice x28 -> x0, local copies, waits for them, and re-layouts: 10.1 us -> none  [body(): kept = lax.map(per_panel, (channel, received, keep_list))]
    convert_element_type x18 -> x1, other arithmetic: 4.92 us -> 0.64 us  [body(): (jnp.arange(devices * capacity)[:, None] == target[None, :]).astype(jnp.b...]
where the time goes in v1:
time: 85.9 us; the launch traced here: 85.3 us
  Pallas kernels  31.4 us (37%)
  waiting for transfers between devices  21.1 us (25%)
  blocking collectives  17.7 us (21%)
  starting transfers between devices  8.42 us (10%)
  local copies, waits for them, and re-layouts  4.84 us (6%)
  other arithmetic  1.73 us (2%)
    pallas_call x1, Pallas kernels, panel_sums(): pl.pallas_call(kernel, grid_spec=pltpu.PrefetchScalarGridSpec(num_scalar_...  22.6 us
    all_to_all x1, waiting for transfers between devices, body(): lax.all_to_all(parts, 'panel', split_axis=0, concat_axis=0, tiled=True)  21.1 us
    all_to_all x1, blocking collectives, body(): lax.all_to_all(shaped, ('panel', 'prb'), split_axis=0, concat_axis=0, til...  17.7 us
    pallas_call x1, Pallas kernels, solve_and_route(): pl.pallas_call(functools.partial(solve_kernel, sources=arrived.shape[0]),...  8.8 us
    all_to_all x1, starting transfers between devices, body(): lax.all_to_all(parts, 'panel', split_axis=0, concat_axis=0, tiled=True)  8.42 us
  transfers between devices with their start and end apart: 1, of which 1 were waited for; matrix products, arithmetic and copies ran while one was open for 2% of the time, Pallas kernels for 0%

profile of v1, /device:TPU:1, one launch (start us, length us, event | category | flops | bytes accessed | tf_op | source)
XLA Modules:
  0.0 85.3 jit_solution(7448370205791224448)
XLA Ops:
  0.0 0.0 copy-start
  0.0 0.8 select_reduce_fusion.2
  0.8 0.7 reshape.30.pats_ref
  1.4 22.6 %panel_sums.1 = bf16[32,64,384]{2,1,0:T(8,128)(2,1)} custom-call(s32[448]{0:T(512)} %reshape.30.pats_ref, bf16[2,16,64,256]{3,2,1,0:T(8,128)(2,1)} %constant.27.clone.table_ref, bf16[14,32,64,128]{3,2,1,0:T(8,128)(2,1)} %ch_ref.1, bf16[14,32,64,288]{3,2,1,0:T(8,128)(2,1)} %rx_ref.1), custom_call_target="tpu_custom_call" | custom-call | tf_op jit(solution)/shard_map/panel_sums/pallas_call | solution.py:92
  24.1 8.4 %all-to-all-start = ((bf16[16,2,64,384]{3,2,1,0:T(8,128)(2,1)}), bf16[16,2,64,384]{3,2,1,0:T(8,128)(2,1)S(1)}, u32[]{:S(2)}, u32[]{:S(2)}) async-start(bf16[16,2,64,384]{3,2,1,0:T(8,128)(2,1)} %bitcast.3), calls=%async_computation | async-start | bytes 3145728 | tf_op jit(solution)/shard_map/all_to_all | solution.py:171
  32.5 0.0 copy-done
  32.5 0.1 constant_dynamic-slice_fusion.1
  32.6 0.1 copy.14
  32.7 0.0 copy-done.3
  32.7 0.2 select_reduce_fusion
  32.9 0.6 reshape.32.noise_ref
  33.4 0.0 copy-done.2
  33.4 0.1 constant_dynamic-slice_fusion
  33.6 0.1 copy.15
  33.6 0.1 reshape.33
  33.7 0.1 select_reduce_fusion.1
  33.9 0.6 fusion.place_ref
  34.5 21.1 %all-to-all-done.arr_ref = bf16[16,2,64,384]{3,2,1,0:T(8,128)(2,1)S(1)} async-done(((bf16[16,2,64,384]{3,2,1,0:T(8,128)(2,1)}), bf16[16,2,64,384]{3,2,1,0:T(8,128)(2,1)S(1)}, u32[]{:S(2)}, u32[]{:S(2)}) %all-to-all-start) | async-done | bytes 1572896 | tf_op jit(solution)/shard_map/all_to_all | solution.py:171
  55.6 1.2 %copy-done.1 = bf16[16,2,64,384]{3,2,1,0:T(8,128)(2,1)} copy-done((bf16[16,2,64,384]{3,2,1,0:T(8,128)(2,1)}, bf16[16,2,64,384]{3,2,1,0:T(8,128)(2,1)S(1)}, u32[]{:S(2)}) %copy-start.1) | copy-done | bytes 1572888
  56.8 8.8 %solve_and_route.1 = bf16[256,288]{1,0:T(8,128)(2,1)} custom-call(bf16[16,2,64,384]{3,2,1,0:T(8,128)(2,1)} %copy-done.1, f32[1,128]{1,0:T(1,128)} %reshape.32.noise_ref, bf16[256,128]{1,0:T(8,128)(2,1)} %fusion.place_ref), custom_call_target="tpu_custom_call" | custom-call | tf_op jit(solution)/shard_map/solve_and_route/pallas_call | solution.py:156
  65.6 1.0 %reshape.34 = bf16[128,2,288]{2,1,0:T(2,128)(2,1)S(1)} reshape(bf16[256,288]{1,0:T(8,128)(2,1)} %solve_and_route.1) | data formatting | bytes 294912 | tf_op jit(solution)/shard_map/reshape | solution.py:189
  66.6 17.7 %all_to_all.10 = bf16[128,2,288]{2,1,0:T(2,128)(2,1)S(1)} all-to-all(bf16[128,2,288]{2,1,0:T(2,128)(2,1)S(1)} %reshape.34), channel_id=1, replica_groups=mesh['panel'=16,'prb'=8] {'panel','prb'}, dimensions={0} | all-to-all | bytes 294912 | tf_op jit(solution)/shard_map/all_to_all | solution.py:190
  84.3 0.1 reshape.35
  84.4 0.9 %copy.16 = f32[256,288]{0,1:T(8,128)} copy(f32[256,288]{1,0:T(8,128)S(1)} %reshape.35) | data formatting | bytes 589824 | tf_op jit(solution)/shard_map/convert_element_type | solution.py:191
  (4 shorter events, 0.0 us)
Async XLA Ops:
  0.0 32.5 %copy-start = (s32[256,64]{0,1:T(8,128)S(1)}, s32[256,64]{0,1:T(8,128)}, u32[]{:S(2)}) copy-start(s32[256,64]{0,1:T(8,128)} %param.10) | copy-start | bytes 196612
  1.4 31.2 %copy-start.3 = (f32[512]{0:T(512)S(1)}, f32[512]{0:T(512)}, u32[]{:S(2)}) copy-start(f32[512]{0:T(512)} %param.11) | copy-start | bytes 6148
  1.4 32.0 %copy-start.2 = (s32[256,64,1]{0,2,1:T(1,128)S(1)}, s32[256,64,1]{0,2,1:T(1,128)}, u32[]{:S(2)}) copy-start(s32[256,64,1]{0,2,1:T(1,128)} %param.12) | copy-start | bytes 196612
  24.1 31.5 %all-to-all-start = ((bf16[16,2,64,384]{3,2,1,0:T(8,128)(2,1)}), bf16[16,2,64,384]{3,2,1,0:T(8,128)(2,1)S(1)}, u32[]{:S(2)}, u32[]{:S(2)}) async-start(bf16[16,2,64,384]{3,2,1,0:T(8,128)(2,1)} %bitcast.3), calls=%async_computation | async-start | bytes 3145728 | tf_op jit(solution)/shard_map/all_to_all | solution.py:171
  55.6 1.2 %copy-start.1 = (bf16[16,2,64,384]{3,2,1,0:T(8,128)(2,1)}, bf16[16,2,64,384]{3,2,1,0:T(8,128)(2,1)S(1)}, u32[]{:S(2)}) copy-start(bf16[16,2,64,384]{3,2,1,0:T(8,128)(2,1)S(1)} %all-to-all-done.arr_ref) | copy-start | bytes 4718596

commit v2 on v1

--- a/solution.py
+++ b/solution.py
@@ -1,3 +1,5 @@
+import functools
+
 import jax
 import jax.numpy as jnp
 import ml_dtypes
@@ -42,69 +44,156 @@
     return jnp.concatenate([m[:, width:], -m[:, :width]], axis=1)
 
 
-def sums_kernel(pats_ref, table_ref, ch_ref, rx_ref, out_ref, *, panels, prbs, steps_prb):
-    step = pl.program_id(0)
-    for j in range(prbs):
-        p = step * prbs + j
-        pieces = []
-        for n in range(0, panels, 2):
-            pair = ch_ref[n : n + 2, j].reshape(2 * ANT, 2 * LAYERS)
-            weights = jnp.concatenate(
-                [
-                    table_ref[0, pats_ref[n * steps_prb + p]],
-                    table_ref[1, pats_ref[(n + 1) * steps_prb + p]],
-                ],
-                axis=0,
+def sums_kernel(
+    pats_ref, table_hbm, ch_hbm, rx_hbm, out_hbm, table_ref, ch_buf, rx_buf, out_buf, table_sem,
+    in_sems, out_sems, *, panels, pieces, prbs,
+):
+    def incoming(i):
+        rows = pl.ds(i * prbs, prbs)
+        return (
+            pltpu.make_async_copy(ch_hbm.at[:, rows], ch_buf.at[:, rows], in_sems.at[0, i]),
+            pltpu.make_async_copy(rx_hbm.at[:, rows], rx_buf.at[:, rows], in_sems.at[1, i]),
+        )
+
+    def leaving(i):
+        rows = pl.ds(i * prbs, prbs)
+        return pltpu.make_async_copy(out_buf.at[rows], out_hbm.at[rows], out_sems.at[i])
+
+    table_copy = pltpu.make_async_copy(table_hbm, table_ref, table_sem)
+    for i in range(pieces):
+        if i == 0:
+            table_copy.start()
+        for copy in incoming(i):
+            copy.start()
+    table_copy.wait()
+    row = lax.broadcasted_iota(jnp.int32, (LAYERS, 128), 0)
+    lane = lax.broadcasted_iota(jnp.int32, (LAYERS, 128), 1)
+
+    def piece(i, carry):
+        for copy in incoming(i):
+            copy.wait()
+        for j in range(prbs):
+            local = i * prbs + j
+            pieces_t = []
+            for n in range(0, panels, 2):
+                pair = ch_buf[n : n + 2, local].reshape(2 * ANT, 2 * LAYERS)
+                weights = jnp.concatenate(
+                    [
+                        table_ref[0, pats_ref[n, local]],
+                        table_ref[1, pats_ref[n + 1, local]],
+                    ],
+                    axis=0,
+                )
+                ab = jnp.dot(pair.T, weights, preferred_element_type=jnp.float32)
+                a, b = ab[:, : 2 * ANT], ab[:, 2 * ANT :]
+                pieces_t.append(
+                    jnp.concatenate(
+                        [a[:LAYERS] + b[LAYERS:], a[LAYERS:] - b[:LAYERS]], axis=0
+                    ).astype(jnp.bfloat16)
+                )
+            left = jnp.concatenate(pieces_t, axis=1)
+            ch = ch_buf[:, local].reshape(panels * ANT, 2 * LAYERS)
+            rx = rx_buf[:, local].reshape(panels * ANT, 2 * RES)
+            head = jnp.dot(left, rx[:, :256], preferred_element_type=jnp.float32)
+            rest = jnp.dot(
+                left, jnp.concatenate([ch, rx[:, 256:]], axis=1), preferred_element_type=jnp.float32
             )
-            ab = jnp.dot(pair.T, weights, preferred_element_type=jnp.float32)
-            a, b = ab[:, : 2 * ANT], ab[:, 2 * ANT :]
-            pieces.append(
-                jnp.concatenate(
-                    [a[:LAYERS] + b[LAYERS:], a[LAYERS:] - b[:LAYERS]], axis=0
-                ).astype(jnp.bfloat16)
-            )
-        left = jnp.concatenate(pieces, axis=1)
-        ch = ch_ref[:, j].reshape(panels * ANT, 2 * LAYERS)
-        rx = rx_ref[:, j].reshape(panels * ANT, 2 * RES)
-        head = jnp.dot(left, rx[:, :256], preferred_element_type=jnp.float32)
-        rest = jnp.dot(
-            left, jnp.concatenate([ch, rx[:, 256:]], axis=1), preferred_element_type=jnp.float32
-        )
-        my = jnp.concatenate([head, rest[:, 128:]], axis=1)
-        mh = rest[:, :128]
-        z = my[:LAYERS] + rotated(my[LAYERS:], RES)
-        g = mh[:LAYERS] + rotated(mh[LAYERS:], LAYERS)
-        swapped = pltpu.roll(g, LAYERS, axis=1)
-        row = lax.broadcasted_iota(jnp.int32, (LAYERS, 128), 0)
-        lane = lax.broadcasted_iota(jnp.int32, (LAYERS, 128), 1)
-        packed = jnp.where(row >= lane - LAYERS, swapped, g)
-        out_ref[j, :, :256] = z[:, :256].astype(jnp.bfloat16)
-        tail = jnp.concatenate([z[:, 256:], jnp.zeros((LAYERS, 96), jnp.float32)], axis=1)
-        out_ref[j, :, 256:] = jnp.where(lane >= LAYERS, packed, tail).astype(jnp.bfloat16)
-
-
-def panel_sums(pats, channel, received):
+            my = jnp.concatenate([head, rest[:, 128:]], axis=1)
+            mh = rest[:, :128]
+            z = my[:LAYERS] + rotated(my[LAYERS:], RES)
+            g = mh[:LAYERS] + rotated(mh[LAYERS:], LAYERS)
+            swapped = pltpu.roll(g, LAYERS, axis=1)
+            packed = jnp.where(row >= lane - LAYERS, swapped, g)
+            tail = jnp.concatenate([z[:, 256:], jnp.zeros((LAYERS, 96), jnp.float32)], axis=1)
+            out_buf[local, :, :256] = z[:, :256].astype(out_buf.dtype)
+            out_buf[local, :, 256:] = jnp.where(lane >= LAYERS, packed, tail).astype(out_buf.dtype)
+        leaving(i).start()
+        return carry
+
+    lax.fori_loop(0, pieces, piece, 0)
+    for i in range(pieces):
+        leaving(i).wait()
+
+
+def panel_sums(pats, channel, received, prbs=4):
     panels, prb_local = channel.shape[:2]
-    prbs = 2
-    import functools
-
-    kernel = functools.partial(sums_kernel, panels=panels, prbs=prbs, steps_prb=prb_local)
+    pieces = prb_local // prbs
+    kernel = functools.partial(sums_kernel, panels=panels, pieces=pieces, prbs=prbs)
     return pl.pallas_call(
         kernel,
         grid_spec=pltpu.PrefetchScalarGridSpec(
             num_scalar_prefetch=1,
-            grid=(prb_local // prbs,),
-            in_specs=[
-                pl.BlockSpec(TABLE.shape, lambda i, s: (0, 0, 0, 0)),
-                pl.BlockSpec((panels, prbs, ANT, 2 * LAYERS), lambda i, s: (0, i, 0, 0)),
-                pl.BlockSpec((panels, prbs, ANT, 2 * RES), lambda i, s: (0, i, 0, 0)),
+            grid=(1,),
+            in_specs=[pl.BlockSpec(memory_space=pl.ANY)] * 3,
+            out_specs=pl.BlockSpec(memory_space=pl.ANY),
+            scratch_shapes=[
+                pltpu.VMEM(TABLE.shape, jnp.bfloat16),
+                pltpu.VMEM((panels, prb_local, ANT, 2 * LAYERS), jnp.bfloat16),
+                pltpu.VMEM((panels, prb_local, ANT, 2 * RES), jnp.bfloat16),
+                pltpu.VMEM((prb_local, LAYERS, PACK), jnp.bfloat16),
+                pltpu.SemaphoreType.DMA(()),
+                pltpu.SemaphoreType.DMA((2, pieces)),
+                pltpu.SemaphoreType.DMA((pieces,)),
             ],
-            out_specs=pl.BlockSpec((prbs, LAYERS, PACK), lambda i, s: (i, 0, 0)),
         ),
         out_shape=jax.ShapeDtypeStruct((prb_local, LAYERS, PACK), jnp.bfloat16),
         compiler_params=pltpu.CompilerParams(dimension_semantics=("arbitrary",)),
         name="panel_sums",
     )(pats, jnp.asarray(TABLE), channel, received)
+
+
+TILE = 8
+GROUP = 4
+
+
+def less_product(acc, left, right):
+    return (
+        acc[0] - (left[0] * right[0] - left[1] * right[1]),
+        acc[1] - (left[0] * right[1] + left[1] * right[0]),
+    )
+
+
+def inverse_tiles(tiles, col, base):
+    count = len(tiles) * TILE
+    row = lax.broadcasted_iota(jnp.int32, col.shape, 0)
+    for k in range(0, count, GROUP):
+        spread = []
+        for j in range(GROUP):
+            idx = base + (k + j)
+            spread.append(
+                [
+                    tuple(
+                        jnp.take_along_axis(part, idx, axis=1, mode="promise_in_bounds")
+                        for part in tile
+                    )
+                    for tile in tiles
+                ]
+            )
+        for j in range(GROUP):
+            at = k + j
+            t, r = at // TILE, at % TILE
+            here = col == at
+            this = row == r
+            column = spread[j]
+            inv = 1.0 / column[t][0][r : r + 1]
+            pivot = (
+                jnp.where(here[:1], inv, tiles[t][0][r : r + 1] * inv),
+                jnp.where(here[:1], 0.0, tiles[t][1][r : r + 1] * inv),
+            )
+            tiles = [
+                less_product(tuple(jnp.where(here, 0.0, part) for part in tile), c, pivot)
+                for tile, c in zip(tiles, column)
+            ]
+            tiles[t] = tuple(jnp.where(this, p, part) for p, part in zip(pivot, tiles[t]))
+            for other in range(j + 1, GROUP):
+                scale = tuple(part[r : r + 1] * inv for part in spread[other][t])
+                spread[other] = [
+                    less_product(tile, c, scale) for tile, c in zip(spread[other], column)
+                ]
+                spread[other][t] = tuple(
+                    jnp.where(this, s, part) for s, part in zip(scale, spread[other][t])
+                )
+    return tiles
 
 
 def solve_kernel(arr_ref, noise_ref, place_ref, out_ref, *, sources):
@@ -125,21 +214,10 @@
     ar = jnp.where(row >= col, q, qt) + jnp.where(row == col, noise_ref[...], 0.0)
     ai = jnp.where(col > row, q, jnp.where(col < row, -qt, 0.0))
     base = jnp.where(upper, LAYERS, 0)
-    for k in range(LAYERS):
-        idx = base + k
-        cr = jnp.take_along_axis(ar, idx, axis=1, mode="promise_in_bounds")
-        ci = jnp.take_along_axis(ai, idx, axis=1, mode="promise_in_bounds")
-        inv = 1.0 / cr[k : k + 1]
-        here = col == k
-        ar = jnp.where(here, 0.0, ar)
-        ai = jnp.where(here, 0.0, ai)
-        rr = jnp.where(here[:1], inv, ar[k : k + 1] * inv)
-        ri = ai[k : k + 1] * inv
-        ar = ar - (cr * rr - ci * ri)
-        ai = ai - (cr * ri + ci * rr)
-        this = row == k
-        ar = jnp.where(this, rr, ar)
-        ai = jnp.where(this, ri, ai)
+    tiles = [(ar[i : i + TILE], ai[i : i + TILE]) for i in range(0, LAYERS, TILE)]
+    tiles = inverse_tiles(tiles, col[:TILE], base[:TILE])
+    ar = jnp.concatenate([tile[0] for tile in tiles], axis=0)
+    ai = jnp.concatenate([tile[1] for tile in tiles], axis=0)
     z = jnp.concatenate([s0[:, : 2 * RES], s1[:, : 2 * RES]], axis=0)
     rows = []
     for half in (~upper, upper):
@@ -151,13 +229,13 @@
 
 
 def solve_and_route(arrived, noise, place):
-    import functools
-
     return pl.pallas_call(
         functools.partial(solve_kernel, sources=arrived.shape[0]),
+        in_specs=[pl.BlockSpec(memory_space=pltpu.VMEM)] * 3,
+        out_specs=pl.BlockSpec(memory_space=pltpu.VMEM),
         out_shape=jax.ShapeDtypeStruct((place.shape[0], 2 * RES), jnp.bfloat16),
         name="solve_and_route",
-    )(arrived, noise, place)
+    )(pltpu.with_memory_space_constraint(arrived, pltpu.VMEM), noise, place)
 
 
 def body(channel, received, keep_list, alloc, noise_var, owner):
@@ -166,7 +244,7 @@
     prb_local = channel.shape[1]
     prb_own = prb_local // panel_count
     pats = jnp.sum(jnp.where(keep_list < NBLK, 1 << keep_list, 0), axis=-1).astype(jnp.int32)
-    sums = panel_sums(pats.reshape(-1), channel, received)
+    sums = panel_sums(pats, channel, received)
     parts = sums.reshape(panel_count, prb_own, LAYERS, PACK)
     arrived = lax.all_to_all(parts, "panel", split_axis=0, concat_axis=0, tiled=True)
 

time: 85.9 us -> 81.7 us (0.951)
  Pallas kernels: 31.4 us -> 28.7 us
  local copies, waits for them, and re-layouts: 4.84 us -> 3.04 us
    pallas_call x1, Pallas kernels: 8.8 us -> 6.38 us  [solve_and_route(): pl.pallas_call(functools.partial(solve_kernel, sources=arrived.shape[0]),...]
    unnamed x8 -> x6, local copies, waits for them, and re-layouts: 1.16 us -> 0.01 us
where the time goes in v2:
time: 81.7 us; the launch traced here: 81.3 us
  Pallas kernels  28.7 us (35%)
  waiting for transfers between devices  21.1 us (26%)
  blocking collectives  17.7 us (22%)
  starting transfers between devices  8.43 us (10%)
  local copies, waits for them, and re-layouts  3.04 us (4%)
  other arithmetic  2.33 us (3%)
    pallas_call x1, Pallas kernels, panel_sums(): pl.pallas_call(kernel, grid_spec=pltpu.PrefetchScalarGridSpec(num_scalar_...  22.3 us
    all_to_all x1, waiting for transfers between devices, body(): lax.all_to_all(parts, 'panel', split_axis=0, concat_axis=0, tiled=True)  21.1 us
    all_to_all x1, blocking collectives, body(): lax.all_to_all(shaped, ('panel', 'prb'), split_axis=0, concat_axis=0, til...  17.7 us
    all_to_all x1, starting transfers between devices, body(): lax.all_to_all(parts, 'panel', split_axis=0, concat_axis=0, tiled=True)  8.43 us
    pallas_call x1, Pallas kernels, solve_and_route(): pl.pallas_call(functools.partial(solve_kernel, sources=arrived.shape[0]),...  6.38 us
  transfers between devices with their start and end apart: 1, of which 1 were waited for; matrix products, arithmetic and copies ran while one was open for 2% of the time, Pallas kernels for 0%

profile of v2, /device:TPU:1, one launch (start us, length us, event | category | flops | bytes accessed | tf_op | source)
XLA Modules:
  0.0 81.3 jit_solution(15703025320387634947)
XLA Ops:
  0.0 0.0 copy-start
  0.0 1.4 %select_reduce_fusion.2.pats_ref = s32[14,32]{1,0:T(8,128)} fusion(s32[14,32,3]{1,0,2:T(8,128)} %param.9), kind=kLoop, calls=%fused_computation.7 | loop fusion | flops 4928 | bytes 7168 | tf_op jit(solution)/shard_map/reduce_sum | solution.py:246
  1.4 0.0 copy-start.2
  1.4 0.0 copy-start.1
  1.4 22.3 %panel_sums.1 = bf16[32,64,384]{2,1,0:T(8,128)(2,1)} custom-call(s32[14,32]{1,0:T(8,128)} %select_reduce_fusion.2.pats_ref, bf16[2,16,64,256]{3,2,1,0:T(8,128)(2,1)} %constant.27.clone.table_hbm, bf16[14,32,64,128]{3,2,1,0:T(8,128)(2,1)} %ch_hbm.1, bf16[14,32,64,288]{3,2,1,0:T(8,128)(2,1)} %rx_hbm.1), custom_call_target="tpu_custom_call" | custom-call | tf_op jit(solution)/shard_map/panel_sums/pallas_call | solution.py:122
  23.7 8.4 %all-to-all-start = ((bf16[16,2,64,384]{3,2,1,0:T(8,128)(2,1)}), bf16[16,2,64,384]{3,2,1,0:T(8,128)(2,1)S(1)}, u32[]{:S(2)}, u32[]{:S(2)}) async-start(bf16[16,2,64,384]{3,2,1,0:T(8,128)(2,1)} %bitcast.3), calls=%async_computation | async-start | bytes 3145728 | tf_op jit(solution)/shard_map/all_to_all | solution.py:249
  32.2 0.0 copy-done
  32.2 0.1 constant_dynamic-slice_fusion.1
  32.3 0.1 copy.14
  32.3 0.0 copy-done.2
  32.3 0.2 select_reduce_fusion
  32.5 0.6 reshape.28.noise_ref
  33.1 0.0 copy-done.1
  33.1 0.1 constant_dynamic-slice_fusion
  33.2 0.1 copy.15
  33.3 0.1 reshape.29
  33.4 0.1 select_reduce_fusion.1
  33.5 0.6 fusion.place_ref
  34.1 21.1 %all-to-all-done.arr_ref = bf16[16,2,64,384]{3,2,1,0:T(8,128)(2,1)S(1)} async-done(((bf16[16,2,64,384]{3,2,1,0:T(8,128)(2,1)}), bf16[16,2,64,384]{3,2,1,0:T(8,128)(2,1)S(1)}, u32[]{:S(2)}, u32[]{:S(2)}) %all-to-all-start) | async-done | bytes 1572896 | tf_op jit(solution)/shard_map/all_to_all | solution.py:249
  55.2 6.4 %solve_and_route.1 = bf16[256,288]{1,0:T(8,128)(2,1)} custom-call(bf16[16,2,64,384]{3,2,1,0:T(8,128)(2,1)S(1)} %all-to-all-done.arr_ref, f32[1,128]{1,0:T(1,128)} %reshape.28.noise_ref, bf16[256,128]{1,0:T(8,128)(2,1)} %fusion.place_ref), custom_call_target="tpu_custom_call" | custom-call | tf_op jit(solution)/shard_map/solve_and_route/pallas_call | solution.py:232
  61.6 1.0 %reshape.30 = bf16[128,2,288]{2,1,0:T(2,128)(2,1)S(1)} reshape(bf16[256,288]{1,0:T(8,128)(2,1)} %solve_and_route.1) | data formatting | bytes 294912 | tf_op jit(solution)/shard_map/reshape | solution.py:267
  62.6 17.7 %all_to_all.10 = bf16[128,2,288]{2,1,0:T(2,128)(2,1)S(1)} all-to-all(bf16[128,2,288]{2,1,0:T(2,128)(2,1)S(1)} %reshape.30), channel_id=1, replica_groups=mesh['panel'=16,'prb'=8] {'panel','prb'}, dimensions={0} | all-to-all | bytes 294912 | tf_op jit(solution)/shard_map/all_to_all | solution.py:268
  80.3 0.1 reshape.31
  80.5 0.9 %copy.16 = f32[256,288]{0,1:T(8,128)} copy(f32[256,288]{1,0:T(8,128)S(1)} %reshape.31) | data formatting | bytes 589824 | tf_op jit(solution)/shard_map/convert_element_type | solution.py:269
  (1 shorter events, 0.0 us)
Async XLA Ops:
  0.0 32.2 %copy-start = (s32[256,64]{0,1:T(8,128)S(1)}, s32[256,64]{0,1:T(8,128)}, u32[]{:S(2)}) copy-start(s32[256,64]{0,1:T(8,128)} %param.10) | copy-start | bytes 196612
  1.4 31.0 %copy-start.2 = (f32[512]{0:T(512)S(1)}, f32[512]{0:T(512)}, u32[]{:S(2)}) copy-start(f32[512]{0:T(512)} %param.11) | copy-start | bytes 6148
  1.4 31.7 %copy-start.1 = (s32[256,64,1]{0,2,1:T(1,128)S(1)}, s32[256,64,1]{0,2,1:T(1,128)}, u32[]{:S(2)}) copy-start(s32[256,64,1]{0,2,1:T(1,128)} %param.12) | copy-start | bytes 196612
  23.7 31.5 %all-to-all-start = ((bf16[16,2,64,384]{3,2,1,0:T(8,128)(2,1)}), bf16[16,2,64,384]{3,2,1,0:T(8,128)(2,1)S(1)}, u32[]{:S(2)}, u32[]{:S(2)}) async-start(bf16[16,2,64,384]{3,2,1,0:T(8,128)(2,1)} %bitcast.3), calls=%async_computation | async-start | bytes 3145728 | tf_op jit(solution)/shard_map/all_to_all | solution.py:249

commit v3 on v2

--- a/solution.py
+++ b/solution.py
@@ -60,18 +60,24 @@
         return pltpu.make_async_copy(out_buf.at[rows], out_hbm.at[rows], out_sems.at[i])
 
     table_copy = pltpu.make_async_copy(table_hbm, table_ref, table_sem)
-    for i in range(pieces):
-        if i == 0:
-            table_copy.start()
-        for copy in incoming(i):
-            copy.start()
+    table_copy.start()
+    for copy in incoming(0):
+        copy.start()
     table_copy.wait()
+    for copy in incoming(1):
+        copy.start()
     row = lax.broadcasted_iota(jnp.int32, (LAYERS, 128), 0)
     lane = lax.broadcasted_iota(jnp.int32, (LAYERS, 128), 1)
 
     def piece(i, carry):
         for copy in incoming(i):
             copy.wait()
+
+        @pl.when(i + 2 < pieces)
+        def _():
+            for copy in incoming(i + 2):
+                copy.start()
+
         for j in range(prbs):
             local = i * prbs + j
             pieces_t = []
@@ -115,7 +121,7 @@
         leaving(i).wait()
 
 
-def panel_sums(pats, channel, received, prbs=4):
+def panel_sums(pats, channel, received, prbs=8):
     panels, prb_local = channel.shape[:2]
     pieces = prb_local // prbs
     kernel = functools.partial(sums_kernel, panels=panels, pieces=pieces, prbs=prbs)
@@ -143,7 +149,7 @@
 
 
 TILE = 8
-GROUP = 4
+GROUP = 8
 
 
 def less_product(acc, left, right):
@@ -229,13 +235,14 @@
 
 
 def solve_and_route(arrived, noise, place):
+    held = [pltpu.with_memory_space_constraint(v, pltpu.VMEM) for v in (arrived, noise, place)]
     return pl.pallas_call(
         functools.partial(solve_kernel, sources=arrived.shape[0]),
         in_specs=[pl.BlockSpec(memory_space=pltpu.VMEM)] * 3,
         out_specs=pl.BlockSpec(memory_space=pltpu.VMEM),
-        out_shape=jax.ShapeDtypeStruct((place.shape[0], 2 * RES), jnp.bfloat16),
+        out_shape=pltpu.VMEM((place.shape[0], 2 * RES), jnp.bfloat16),
         name="solve_and_route",
-    )(pltpu.with_memory_space_constraint(arrived, pltpu.VMEM), noise, place)
+    )(*held)
 
 
 def body(channel, received, keep_list, alloc, noise_var, owner):

time: 81.7 us -> 71.9 us (0.88)
  Pallas kernels: 28.7 us -> 19.9 us
  local copies, waits for them, and re-layouts: 3.04 us -> 1.63 us
  waiting for transfers between devices: 21.1 us -> 22.2 us
    pallas_call x1, Pallas kernels: 22.3 us -> 15.4 us  [panel_sums(): pl.pallas_call(kernel, grid_spec=pltpu.PrefetchScalarGridSpec(num_scalar_...]
    pallas_call x1, Pallas kernels: 6.38 us -> 4.46 us  [solve_and_route(): pl.pallas_call(functools.partial(solve_kernel, sources=arrived.shape[0]),...]
    all_to_all x1, waiting for transfers between devices: 21.1 us -> 22.2 us  [body(): lax.all_to_all(parts, 'panel', split_axis=0, concat_axis=0, tiled=True)]
    reshape x1, local copies, waits for them, and re-layouts: 1.02 us -> 0.1 us  [body(): shaped = outgoing.reshape(devices, capacity, 2 * RES)]
  transfers between devices with their start and end apart: 1 -> 1, of which waited for: 1 -> 1; matrix products, arithmetic and copies ran while one was open for 2% -> 1% of each run, Pallas kernels for 0% -> 0%
where the time goes in v3:
time: 71.9 us; the launch traced here: 71.6 us
  waiting for transfers between devices  22.2 us (31%)
  Pallas kernels  19.9 us (28%)
  blocking collectives  17.7 us (25%)
  starting transfers between devices  8.43 us (12%)
  other arithmetic  1.71 us (2%)
  local copies, waits for them, and re-layouts  1.63 us (2%)
    all_to_all x1, waiting for transfers between devices, body(): lax.all_to_all(parts, 'panel', split_axis=0, concat_axis=0, tiled=True)  22.2 us
    all_to_all x1, blocking collectives, body(): lax.all_to_all(shaped, ('panel', 'prb'), split_axis=0, concat_axis=0, til...  17.7 us
    pallas_call x1, Pallas kernels, panel_sums(): pl.pallas_call(kernel, grid_spec=pltpu.PrefetchScalarGridSpec(num_scalar_...  15.4 us
    all_to_all x1, starting transfers between devices, body(): lax.all_to_all(parts, 'panel', split_axis=0, concat_axis=0, tiled=True)  8.43 us
    pallas_call x1, Pallas kernels, solve_and_route(): pl.pallas_call(functools.partial(solve_kernel, sources=arrived.shape[0]),...  4.46 us
  transfers between devices with their start and end apart: 1, of which 1 were waited for; matrix products, arithmetic and copies ran while one was open for 1% of the time, Pallas kernels for 0%

profile of v3, /device:TPU:1, one launch (start us, length us, event | category | flops | bytes accessed | tf_op | source)
XLA Modules:
  0.0 71.6 jit_solution(16483607828633618792)
XLA Ops:
  0.0 0.0 copy-start
  0.0 1.4 %select_reduce_fusion.2.pats_ref = s32[14,32]{1,0:T(8,128)} fusion(s32[14,32,3]{1,0,2:T(8,128)} %param.9), kind=kLoop, calls=%fused_computation.7 | loop fusion | flops 4928 | bytes 7168 | tf_op jit(solution)/shard_map/reduce_sum | solution.py:253
  1.4 0.0 copy-start.2
  1.4 0.0 copy-start.1
  1.4 15.4 %panel_sums.1 = bf16[32,64,384]{2,1,0:T(8,128)(2,1)} custom-call(s32[14,32]{1,0:T(8,128)} %select_reduce_fusion.2.pats_ref, bf16[2,16,64,256]{3,2,1,0:T(8,128)(2,1)} %constant.27.clone.table_hbm, bf16[14,32,64,128]{3,2,1,0:T(8,128)(2,1)} %ch_hbm.1, bf16[14,32,64,288]{3,2,1,0:T(8,128)(2,1)} %rx_hbm.1), custom_call_target="tpu_custom_call" | custom-call | tf_op jit(solution)/shard_map/panel_sums/pallas_call | solution.py:128
  16.8 8.4 %all-to-all-start = ((bf16[16,2,64,384]{3,2,1,0:T(8,128)(2,1)}), bf16[16,2,64,384]{3,2,1,0:T(8,128)(2,1)S(1)}, u32[]{:S(2)}, u32[]{:S(2)}) async-start(bf16[16,2,64,384]{3,2,1,0:T(8,128)(2,1)} %bitcast.3), calls=%async_computation | async-start | bytes 3145728 | tf_op jit(solution)/shard_map/all_to_all | solution.py:256
  25.3 0.0 copy-done
  25.3 0.1 constant_dynamic-slice_fusion.1
  25.4 0.1 copy.14
  25.4 0.0 copy-done.2
  25.4 0.2 select_reduce_fusion
  25.6 0.1 reshape.28.noise_ref
  25.7 0.0 copy-done.1
  25.7 0.1 constant_dynamic-slice_fusion
  25.8 0.1 copy.15
  25.9 0.1 reshape.29
  26.0 0.1 select_reduce_fusion.1
  26.2 22.2 %all-to-all-done.arr_ref = bf16[16,2,64,384]{3,2,1,0:T(8,128)(2,1)S(1)} async-done(((bf16[16,2,64,384]{3,2,1,0:T(8,128)(2,1)}), bf16[16,2,64,384]{3,2,1,0:T(8,128)(2,1)S(1)}, u32[]{:S(2)}, u32[]{:S(2)}) %all-to-all-start) | async-done | bytes 1572896 | tf_op jit(solution)/shard_map/all_to_all | solution.py:256
  48.4 4.5 %solve_and_route.1 = bf16[256,288]{1,0:T(8,128)(2,1)S(1)} custom-call(bf16[16,2,64,384]{3,2,1,0:T(8,128)(2,1)S(1)} %all-to-all-done.arr_ref, f32[1,128]{1,0:T(1,128)S(1)} %reshape.28.noise_ref, bf16[256,128]{1,0:T(8,128)(2,1)S(1)} %fusion.place_ref), custom_call_target="tpu_custom_call" | custom-call | tf_op jit(solution)/shard_map/solve_and_route/pallas_call | solution.py:239
  52.8 0.1 reshape.30
  52.9 17.7 %all_to_all.10 = bf16[128,2,288]{2,1,0:T(2,128)(2,1)S(1)} all-to-all(bf16[128,2,288]{2,1,0:T(2,128)(2,1)S(1)} %reshape.30), channel_id=1, replica_groups=mesh['panel'=16,'prb'=8] {'panel','prb'}, dimensions={0} | all-to-all | bytes 294912 | tf_op jit(solution)/shard_map/all_to_all | solution.py:275
  70.6 0.1 reshape.31
  70.7 0.9 %copy.16 = f32[256,288]{0,1:T(8,128)} copy(f32[256,288]{1,0:T(8,128)S(1)} %reshape.31) | data formatting | bytes 589824 | tf_op jit(solution)/shard_map/convert_element_type | solution.py:276
  (2 shorter events, 0.0 us)
Async XLA Ops:
  0.0 25.3 %copy-start = (s32[256,64]{0,1:T(8,128)S(1)}, s32[256,64]{0,1:T(8,128)}, u32[]{:S(2)}) copy-start(s32[256,64]{0,1:T(8,128)} %param.10) | copy-start | bytes 196612
  1.4 24.1 %copy-start.2 = (f32[512]{0:T(512)S(1)}, f32[512]{0:T(512)}, u32[]{:S(2)}) copy-start(f32[512]{0:T(512)} %param.11) | copy-start | bytes 6148
  1.4 24.3 %copy-start.1 = (s32[256,64,1]{0,2,1:T(1,128)S(1)}, s32[256,64,1]{0,2,1:T(1,128)}, u32[]{:S(2)}) copy-start(s32[256,64,1]{0,2,1:T(1,128)} %param.12) | copy-start | bytes 196612
  16.8 31.5 %all-to-all-start = ((bf16[16,2,64,384]{3,2,1,0:T(8,128)(2,1)}), bf16[16,2,64,384]{3,2,1,0:T(8,128)(2,1)S(1)}, u32[]{:S(2)}, u32[]{:S(2)}) async-start(bf16[16,2,64,384]{3,2,1,0:T(8,128)(2,1)} %bitcast.3), calls=%async_computation | async-start | bytes 3145728 | tf_op jit(solution)/shard_map/all_to_all | solution.py:256
